TPU v7x, 32 devices: a whole 2x2x4 slice. The times are simulated.
32 devices in a mesh: kpt: 4 (over y, x), pw: 8 (over z, core).
Axes of the slice: x: 2, y: 2, z: 4, core: 2. Of those that a mesh axis runs over, the one named last changes fastest.
Arguments:
- energies: float32 [16, 512], P('kpt', 'pw'), may hold values from 0.5 to 3
- current: float32 [2, 16, 512], P(None, 'kpt', 'pw'), may hold values from -40 to 40
- previous: float32 [2, 16, 512], P(None, 'kpt', 'pw'), may hold values from -6 to 6
- previous_beta: float32 [2], replicated, may hold values from 0.5 to 2
- pair_left: bfloat16 [16, 512, 4096], P('kpt', None, 'pw'), may hold values from -0.09375 to 0.09375
- pair_right: bfloat16 [16, 512, 4096], P('kpt', None, 'pw'), may hold values from -0.25 to 0.25
- screened: bfloat16 [16, 4096, 4096], P('kpt', 'pw'), may hold values from -0.0234375 to 0.0234375
- momentum_index: int32 [16, 16], replicated, may hold values from 0 to 15, each once within a row
Outputs:
- last_vector: float32 [2, 16, 512], P(None, 'kpt', 'pw')
- prior_vector: float32 [2, 16, 512], P(None, 'kpt', 'pw')
- alpha_terms: float32 [2, 3], replicated
- beta_terms: float32 [2, 3], replicated
Inputs may be any that keep to these rules, and one draw needn't show every extreme that they name: Each row of momentum_index names every index from 0 to 15 once.
All inputs are finite; a program needn't handle non-finite values.
Results may differ from a plain program's by a relative error of at most 0.003.
Values may be sent and summed in bfloat16 or wider, within the bound.
A program may use at most 128 MiB of HBM per device.

v0:
```python
import jax
import jax.numpy as jnp
from jax import lax
from jax.sharding import PartitionSpec as P

STEPS = 3


epsilon = 1e-06


def screened_images(density, screened):
    kpoint_rows = lax.all_gather(density, "kpt", axis=0, tiled=True)
    return jnp.einsum(
        "qsg,kvg->qkvs",
        screened,
        lax.all_gather(kpoint_rows, "pw", axis=2, tiled=True),
        preferred_element_type=jnp.float32,
    )


def on_device(
    energies, current, previous, previous_beta, pair_left, pair_right, screened, momentum_index
):
    kpoint_total = momentum_index.shape[0]
    band_total = pair_left.shape[1]
    entries = kpoint_total * band_total
    qcount = screened.shape[0]
    qpoints = lax.axis_index("kpt") * qcount + jnp.arange(qcount, dtype=jnp.int32)
    selector = (momentum_index[None, :, :] == qpoints[:, None, None]).astype(jnp.float32)
    vector, earlier, levels = (current, previous, energies)
    beta_before = previous_beta
    alpha_list = []
    beta_list = []
    for turn_index in range(STEPS):
        rounded = vector.astype(jnp.bfloat16)
        rounded = lax.all_gather(rounded, "pw", axis=2, tiled=True)
        density = jnp.einsum(
            "kcg,vkc->kvg", pair_right, rounded, preferred_element_type=jnp.float32
        ).astype(jnp.bfloat16)
        images = screened_images(density, screened)
        partial_field = jnp.einsum(
            "qjk,qkvs->jvs",
            selector,
            images,
            precision=lax.Precision.HIGHEST,
            preferred_element_type=jnp.float32,
        )
        potential = lax.psum_scatter(partial_field, "kpt", scatter_dimension=0, tiled=True).astype(
            jnp.bfloat16
        )
        partial_direct = jnp.einsum(
            "kcs,kvs->vkc", pair_left, potential, preferred_element_type=jnp.float32
        )
        direct = lax.psum_scatter(partial_direct, "pw", scatter_dimension=2, tiled=True)
        applied = levels[None] * vector - direct - beta_before[:, None, None] * earlier
        vector_own = vector
        cross_sum, square_sum, vector_sum = lax.psum(
            (
                jnp.sum(vector_own * applied, axis=(1, 2)),
                jnp.sum(applied * applied, axis=(1, 2)),
                jnp.sum(vector_own * vector_own, axis=(1, 2)),
            ),
            ("kpt", "pw"),
        )
        alpha_now = cross_sum / entries
        mean_square = (
            square_sum / entries
            - 2.0 * alpha_now * (cross_sum / entries)
            + alpha_now * alpha_now * (vector_sum / entries)
        )
        beta_now = jnp.sqrt(mean_square + epsilon)
        residual = applied - alpha_now[:, None, None] * vector
        earlier = vector
        vector = residual / beta_now[:, None, None]
        beta_before = beta_now
        alpha_list.append(alpha_now)
        beta_list.append(beta_now)
    return (vector, earlier, jnp.stack(alpha_list, axis=1), jnp.stack(beta_list, axis=1))


def solution(mesh):
    return jax.shard_map(
        on_device,
        mesh=mesh,
        in_specs=(
            P("kpt", "pw"),
            P(None, "kpt", "pw"),
            P(None, "kpt", "pw"),
            P(),
            P("kpt", None, "pw"),
            P("kpt", None, "pw"),
            P("kpt", "pw", None),
            P(),
        ),
        out_specs=(P(None, "kpt", "pw"), P(None, "kpt", "pw"), P(), P()),
        check_vma=False,
    )
```

profile of v0, /device:TPU:0, one launch (start us, length us, event | category | flops | bytes accessed | tf_op | source)
XLA Modules:
  0.0 434.1 jit_solution(2461469843560152316)
XLA Ops:
  7.2 0.0 reduce-scatter.10.cloned.1.call-start
  7.3 0.8 convert_element_type.28
  8.1 0.1 copy.33
  8.2 15.9 %all_gather.27 = bf16[2,4,512]{1,0,2:T(2,128)(2,1)S(1)} all-gather(bf16[2,4,64]{1,0,2:T(2,128)(2,1)S(1)} %copy.33), channel_id=1, replica_groups=mesh['kpt'=4,'pw'=8] {'pw'}, dimensions={2}, use_global_device_ids=true | all-gather | bytes 9216 | tf_op jit(solution)/shard_map/all_gather | solution.py:37
  24.1 0.1 copy.34
  24.3 0.4 convolution_convert_fusion.2
  24.7 8.2 %all_gather.28 = bf16[16,2,512]{2,1,0:T(2,128)(2,1)S(1)} all-gather(bf16[4,2,512]{2,1,0:T(2,128)(2,1)S(1)} %convolution_convert_fusion.2), channel_id=1, replica_groups=mesh['kpt'=4,'pw'=8] {'kpt'}, dimensions={0}, use_global_device_ids=true | all-gather | bytes 40960 | tf_op jit(solution)/shard_map/all_gather | solution.py:13
  32.9 14.3 %all_gather.29 = bf16[16,2,4096]{2,0,1:T(8,128)(2,1)S(1)} all-gather(bf16[16,2,512]{2,0,1:T(8,128)(2,1)S(1)} %copy.35), channel_id=1, replica_groups=mesh['kpt'=4,'pw'=8] {'pw'}, dimensions={2}, use_global_device_ids=true | all-gather | bytes 294912 | tf_op jit(solution)/shard_map/all_gather | solution.py:17
  47.2 10.8 %fusion.6 = f32[4,16,2,512]{3,1,0,2:T(8,128)S(1)} fusion(bf16[4,512,4096]{2,1,0:T(8,128)(2,1)} %param.14, bf16[16,2,4096]{2,0,1:T(8,128)(2,1)S(1)} %all_gather.29), kind=kOutput, calls=%fused_computation.6 | convolution fusion | flops 536870912 | bytes 17301504 | tf_op jit(solution)/shard_map/qsg,kvg->qkvs/dot_general | solution.py:14
  58.0 0.3 convolution_bitcast_fusion.2
  58.3 0.1 copy.36
  58.4 16.0 %all-reduce = bf16[16,2,512]{2,1,0:T(2,128)(2,1)S(1)} all-reduce(f32[16,2,512]{2,1,0:T(2,128)S(1)} %copy.36), channel_id=2, replica_groups=mesh['kpt'=4,'pw'=8] {'kpt'}, use_global_device_ids=true, to_apply=%region_0.0.clone | all-reduce | flops 16384 | bytes 98304
  74.5 0.6 dynamic-slice
  75.8 2.3 convolution_bitcast_fusion.5
  78.0 0.4 copy.56
  78.5 1.2 reshape.29
  79.6 0.0 reduce-scatter.12.cloned.1.call-start
  79.7 30.9 %reduce-scatter.10.cloned.1.call-done = f32[64,8]{1,0:T(8,128)} async-done(((f32[512,8]{1,0:T(8,128)}), f32[64,8]{1,0:T(8,128)}) %reduce-scatter.10.cloned.1.call-update) | async-done | bytes 2064
  110.5 0.9 reshape.30
  111.4 0.1 copy.37
  111.6 0.2 multiply_reduce_fusion.7
  111.7 37.8 %all-reduce.5 = (f32[2]{0:T(128)S(1)}, f32[2]{0:T(128)S(1)}, f32[2]{0:T(128)S(1)}) all-reduce(f32[2]{0:T(128)S(1)} %get-tuple-element.24, f32[2]{0:T(128)S(1)} %get-tuple-element.23, f32[2]{0:T(128)S(1)} %get-tuple-element.22), channel_id=1, replica_groups=mesh['kpt'=4,'pw'=8] {'kpt','pw'}, use_global_device_ids=true, to_apply=%region_7.0 | all-reduce | flops 6 | bytes 48 | tf_op jit(solution)/shard_map/psum | solution.py:58
  149.6 0.1 fusion.37
  149.6 0.1 copy.38
  149.8 14.9 %all_gather.30 = bf16[2,4,512]{1,0,2:T(2,128)(2,1)S(1)} all-gather(bf16[2,4,64]{1,0,2:T(2,128)(2,1)S(1)} %copy.38), channel_id=1, replica_groups=mesh['kpt'=4,'pw'=8] {'pw'}, dimensions={2}, use_global_device_ids=true | all-gather | bytes 9216 | tf_op jit(solution)/shard_map/all_gather | solution.py:37
  164.6 0.1 copy.39
  164.8 0.4 convolution_convert_fusion.1
  165.2 9.0 %all_gather.31 = bf16[16,2,512]{2,1,0:T(2,128)(2,1)S(1)} all-gather(bf16[4,2,512]{2,1,0:T(2,128)(2,1)S(1)} %convolution_convert_fusion.1), channel_id=1, replica_groups=mesh['kpt'=4,'pw'=8] {'kpt'}, dimensions={0}, use_global_device_ids=true | all-gather | bytes 40960 | tf_op jit(solution)/shard_map/all_gather | solution.py:13
  174.1 14.4 %all_gather.32 = bf16[16,2,4096]{2,0,1:T(8,128)(2,1)S(1)} all-gather(bf16[16,2,512]{2,0,1:T(8,128)(2,1)S(1)} %copy.40), channel_id=1, replica_groups=mesh['kpt'=4,'pw'=8] {'pw'}, dimensions={2}, use_global_device_ids=true | all-gather | bytes 294912 | tf_op jit(solution)/shard_map/all_gather | solution.py:17
  188.5 10.8 %fusion.9 = f32[4,16,2,512]{3,1,0,2:T(8,128)S(1)} fusion(bf16[4,512,4096]{2,1,0:T(8,128)(2,1)} %param.14, bf16[16,2,4096]{2,0,1:T(8,128)(2,1)S(1)} %all_gather.32), kind=kOutput, calls=%fused_computation.7 | convolution fusion | flops 536870912 | bytes 17301504 | tf_op jit(solution)/shard_map/qsg,kvg->qkvs/dot_general | solution.py:14
  199.3 0.4 convolution_bitcast_fusion.1
  199.6 0.1 copy.41
  199.7 15.9 %all-reduce.1 = bf16[16,2,512]{2,1,0:T(2,128)(2,1)S(1)} all-reduce(f32[16,2,512]{2,1,0:T(2,128)S(1)} %copy.41), channel_id=4, replica_groups=mesh['kpt'=4,'pw'=8] {'kpt'}, use_global_device_ids=true, to_apply=%region_8.0.clone | all-reduce | flops 16384 | bytes 98304
  215.7 2.2 convolution_bitcast_fusion.4
  217.9 0.4 copy.58
  218.3 1.2 reshape.31
  219.5 0.0 reduce-scatter.14.cloned.1.call-start
  219.6 29.0 %reduce-scatter.12.cloned.1.call-done = f32[64,8]{1,0:T(8,128)} async-done(((f32[512,8]{1,0:T(8,128)}), f32[64,8]{1,0:T(8,128)}) %reduce-scatter.12.cloned.1.call-update) | async-done | bytes 2064
  248.5 0.9 reshape.32
  249.4 0.1 copy.42
  249.5 0.2 multiply_reduce_fusion.4
  249.7 37.8 %all-reduce.4 = (f32[2]{0:T(128)S(1)}, f32[2]{0:T(128)S(1)}, f32[2]{0:T(128)S(1)}) all-reduce(f32[2]{0:T(128)S(1)} %get-tuple-element.21, f32[2]{0:T(128)S(1)} %get-tuple-element.20, f32[2]{0:T(128)S(1)} %get-tuple-element.19), channel_id=1, replica_groups=mesh['kpt'=4,'pw'=8] {'kpt','pw'}, use_global_device_ids=true, to_apply=%region_15.0 | all-reduce | flops 6 | bytes 48 | tf_op jit(solution)/shard_map/psum | solution.py:58
  287.5 0.1 fusion.36
  287.6 0.1 copy.43
  287.7 14.9 %all_gather.33 = bf16[2,4,512]{1,0,2:T(2,128)(2,1)S(1)} all-gather(bf16[2,4,64]{1,0,2:T(2,128)(2,1)S(1)} %copy.43), channel_id=1, replica_groups=mesh['kpt'=4,'pw'=8] {'pw'}, dimensions={2}, use_global_device_ids=true | all-gather | bytes 9216 | tf_op jit(solution)/shard_map/all_gather | solution.py:37
  302.6 0.1 copy.44
  302.8 0.4 convolution_convert_fusion
  303.1 9.0 %all_gather.34 = bf16[16,2,512]{2,1,0:T(2,128)(2,1)S(1)} all-gather(bf16[4,2,512]{2,1,0:T(2,128)(2,1)S(1)} %convolution_convert_fusion), channel_id=1, replica_groups=mesh['kpt'=4,'pw'=8] {'kpt'}, dimensions={0}, use_global_device_ids=true | all-gather | bytes 40960 | tf_op jit(solution)/shard_map/all_gather | solution.py:13
  312.1 14.2 %all_gather.35 = bf16[16,2,4096]{2,0,1:T(8,128)(2,1)S(1)} all-gather(bf16[16,2,512]{2,0,1:T(8,128)(2,1)S(1)} %copy.45), channel_id=1, replica_groups=mesh['kpt'=4,'pw'=8] {'pw'}, dimensions={2}, use_global_device_ids=true | all-gather | bytes 294912 | tf_op jit(solution)/shard_map/all_gather | solution.py:17
  326.3 10.8 %fusion.12 = f32[4,16,2,512]{3,1,0,2:T(8,128)S(1)} fusion(bf16[4,512,4096]{2,1,0:T(8,128)(2,1)} %param.14, bf16[16,2,4096]{2,0,1:T(8,128)(2,1)S(1)} %all_gather.35), kind=kOutput, calls=%fused_computation.8 | convolution fusion | flops 536870912 | bytes 17301504 | tf_op jit(solution)/shard_map/qsg,kvg->qkvs/dot_general | solution.py:14
  337.1 0.4 convolution_bitcast_fusion
  337.4 0.1 copy.46
  337.5 16.1 %all-reduce.2 = bf16[16,2,512]{2,1,0:T(2,128)(2,1)S(1)} all-reduce(f32[16,2,512]{2,1,0:T(2,128)S(1)} %copy.46), channel_id=6, replica_groups=mesh['kpt'=4,'pw'=8] {'kpt'}, use_global_device_ids=true, to_apply=%region_16.0.clone | all-reduce | flops 16384 | bytes 98304
  353.6 2.2 convolution_bitcast_fusion.3
  355.9 0.4 copy.60
  356.3 1.2 reshape.33
  357.5 29.0 %reduce-scatter.14.cloned.1.call-done = f32[64,8]{1,0:T(8,128)} async-done(((f32[512,8]{1,0:T(8,128)}), f32[64,8]{1,0:T(8,128)}) %reduce-scatter.14.cloned.1.call-update) | async-done | bytes 2064
  386.5 0.9 reshape.34
  387.4 0.1 copy.47
  387.5 0.2 multiply_reduce_fusion.1
  387.7 37.9 %all-reduce.3 = (f32[2]{0:T(128)S(1)}, f32[2]{0:T(128)S(1)}, f32[2]{0:T(128)S(1)}) all-reduce(f32[2]{0:T(128)S(1)} %get-tuple-element.18, f32[2]{0:T(128)S(1)} %get-tuple-element.17, f32[2]{0:T(128)S(1)} %get-tuple-element.16), channel_id=1, replica_groups=mesh['kpt'=4,'pw'=8] {'kpt','pw'}, use_global_device_ids=true, to_apply=%region_23.0 | all-reduce | flops 6 | bytes 48 | tf_op jit(solution)/shard_map/psum | solution.py:58
  425.6 0.6 copy.48
  426.3 0.6 copy.49
  426.9 0.7 subtract_divide_fusion
  (28 shorter events, 0.2 us)
Async XLA Ops:
  7.2 17.1 %copy-start = (bf16[4,512,512]{2,1,0:T(8,128)(2,1)S(1)}, bf16[4,512,512]{2,1,0:T(8,128)(2,1)}, u32[]{:S(2)}) copy-start(bf16[4,512,512]{2,1,0:T(8,128)(2,1)} %param.13) | copy-start | bytes 6291460
  7.2 103.4 %reduce-scatter.10.cloned.1.call-start = ((), (), s32[]{:S(2)}) async-start(), calls=%async_computation.3 | async-start | bytes 294912
  47.2 10.8 %copy-start.1 = (s32[16,16]{1,0:T(8,128)S(1)}, s32[16,16]{1,0:T(8,128)}, u32[]{:S(2)}) copy-start(s32[16,16]{1,0:T(8,128)} %param.15) | copy-start | bytes 3076
  47.2 27.3 %copy-start.7 = (u32[32]{0:T(128)S(1)}, u32[32]{0:T(128)}, u32[]{:S(2)}) copy-start(u32[32]{0:T(128)} %constant.29) | copy-start | bytes 388
  75.7 35.8 %copy-start.2 = (f32[2,4,64]{2,1,0:T(4,128)S(1)}, f32[2,4,64]{2,1,0:T(4,128)}, u32[]{:S(2)}) copy-start(f32[2,4,64]{2,1,0:T(4,128)} %param.9) | copy-start | bytes 6148
  75.7 35.8 %copy-start.4 = (f32[4,64]{1,0:T(4,128)S(1)}, f32[4,64]{1,0:T(4,128)}, u32[]{:S(2)}) copy-start(f32[4,64]{1,0:T(4,128)} %param.8) | copy-start | bytes 3076
  75.7 35.8 %copy-start.5 = (f32[2,4,64]{2,1,0:T(4,128)S(1)}, f32[2,4,64]{2,1,0:T(4,128)}, u32[]{:S(2)}) copy-start(f32[2,4,64]{2,1,0:T(4,128)} %param.10) | copy-start | bytes 6148
  75.8 35.8 %copy-start.6 = (f32[2]{0:T(128)S(1)}, f32[2]{0:T(128)}, u32[]{:S(2)}) copy-start(f32[2]{0:T(128)} %param.11) | copy-start | bytes 28
  79.6 168.9 %reduce-scatter.12.cloned.1.call-start = ((), (), s32[]{:S(2)}) async-start(), calls=%async_computation.4 | async-start | bytes 294912
  219.5 167.0 %reduce-scatter.14.cloned.1.call-start = ((), (), s32[]{:S(2)}) async-start(), calls=%async_computation.5 | async-start | bytes 294912
  287.6 139.3 %copy-start.3 = (f32[2,4,64]{2,1,0:T(4,128)}, f32[2,4,64]{2,1,0:T(4,128)S(1)}, u32[]{:S(2)}) copy-start(f32[2,4,64]{2,1,0:T(4,128)S(1)} %get-tuple-element.36) | copy-start | bytes 6148
Sparse Core Ops, SparseCore 0:
  79.8 30.7 reduce-scatter.9
  219.6 28.8 reduce-scatter.11
  357.6 28.8 reduce-scatter.13
where the time goes:
time: 436 us; the launch traced here: 434 us
  blocking collectives  276 us (63%)
  waiting for transfers between devices  88.9 us (20%)
  matrix products  41.3 us (9%)
  between operations  14.7 us (3%)
  local copies, waits for them, and re-layouts  10.6 us (2%)
    psum x3, blocking collectives, on_device(): lax.psum((jnp.sum(vector_own * applied, axis=(1, 2)), jnp.sum(applied * a...  114 us
    unnamed x6, waiting for transfers between devices  88.9 us
    unnamed x3, blocking collectives  48.1 us
    all_gather x3, blocking collectives, on_device(): rounded = lax.all_gather(rounded, 'pw', axis=2, tiled=True)  45.6 us
    all_gather x3, blocking collectives, screened_images(): lax.all_gather(kpoint_rows, 'pw', axis=2, tiled=True)  42.9 us
    dot_general x3, matrix products, screened_images(): jnp.einsum('qsg,kvg->qkvs', screened, lax.all_gather(kpoint_rows, 'pw', a...  32.4 us
    all_gather x3, blocking collectives, screened_images(): kpoint_rows = lax.all_gather(density, 'kpt', axis=0, tiled=True)  26.1 us
    unnamed x28, local copies, waits for them, and re-layouts  9.32 us
  transfers between devices with their start and end apart: 3, of which 3 were waited for; matrix products, arithmetic and copies ran while one was open for 0% of the time, Pallas kernels for 0%

commit v1 on v0

v1 whole, which is shorter than its diff:
```python
import functools

import jax
import jax.numpy as jnp
from jax import lax
from jax.experimental import pallas as pl
from jax.experimental.pallas import tpu as pltpu
from jax.sharding import PartitionSpec as P

STEPS = 3
LANES = 128

epsilon = 1e-06


def partner(me, i, n):
    i = jnp.int32(i)
    out = jnp.int32(0)
    bit = 1
    while bit < n:
        out = out + lax.rem(lax.div(me, bit) + lax.div(i, bit), 2) * bit
        bit *= 2
    return out


def exchange(buf, axis, n, me, i, send_sem, recv_sem, src=None):
    return pltpu.make_async_remote_copy(
        src_ref=buf.at[me] if src is None else src,
        dst_ref=buf.at[me],
        send_sem=send_sem.at[i],
        recv_sem=recv_sem.at[i],
        device_id={axis: partner(me, i, n)},
        device_id_type=pl.DeviceIdType.MESH,
    )


def arrival(buf, axis, n, me, i, send_sem, recv_sem):
    slot = partner(me, i, n)
    return pltpu.make_async_remote_copy(
        src_ref=buf.at[slot],
        dst_ref=buf.at[slot],
        send_sem=send_sem.at[i],
        recv_sem=recv_sem.at[i],
        device_id={axis: slot},
        device_id_type=pl.DeviceIdType.MESH,
    )


def kernel(
    dims,
    packed_ref, beta_ref, choose_ref, right_hbm, left_hbm, screened_hbm,
    vec_ref, early_ref, coef_ref,
    right, left, screened, packs, first, later, final, dens, images, held, fields, directs,
    dfull, applied_ref, energy_ref, acc,
    right_sem, left_sem, screened_sem,
    pack_s, pack_r, kdens_s, kdens_r, gdens_s, gdens_r, field_s, field_r,
    direct_s, direct_r, final_s, final_r,
):
    nkp, npw, kl, nv, bands, gs = dims
    rows = kl * nv
    total = rows * nkp
    entries = total // nv * bands
    kme = lax.axis_index("kpt")
    pme = lax.axis_index("pw")

    right_copy = pltpu.make_async_copy(right_hbm, right, right_sem)
    left_copy = pltpu.make_async_copy(left_hbm, left, left_sem)

    def screened_copy(i):
        chunk = partner(pme, i, npw)
        start = pl.multiple_of(chunk * gs, gs)
        return pltpu.make_async_copy(
            screened_hbm.at[:, :, pl.ds(start, gs)], screened.at[chunk], screened_sem.at[i]
        )

    right_copy.start()
    for i in range(npw):
        screened_copy(i).start()
    left_copy.start()

    barrier = pltpu.get_barrier_semaphore()
    for axis, n, me in (("kpt", nkp, kme), ("pw", npw, pme)):
        for i in range(1, n):
            pl.semaphore_signal(
                barrier, inc=1, device_id={axis: partner(me, i, n)},
                device_id_type=pl.DeviceIdType.MESH,
            )
    packs[pme] = packed_ref[...]
    pl.semaphore_wait(barrier, nkp - 1 + npw - 1)

    pending = []

    def send_all(buf, axis, n, me, ssem, rsem):
        for i in range(1, n):
            copy = exchange(buf, axis, n, me, i, ssem, rsem)
            copy.start()
            pending.append(copy)

    def wait_all(buf, axis, n, me, ssem, rsem):
        for i in range(1, n):
            arrival(buf, axis, n, me, i, ssem, rsem).wait_recv()

    send_all(packs, "pw", npw, pme, pack_s, pack_r)
    wait_all(packs, "pw", npw, pme, pack_s, pack_r)

    per = npw * LANES // bands
    whole = jnp.concatenate(
        [sum(packs[m * per + j] for j in range(per)) for m in range(bands // LANES)], axis=1
    )
    vec_ref[...] = whole[:rows]
    early_ref[...] = whole[rows : 2 * rows]
    energy_ref[...] = whole[2 * rows :]
    coef_ref[...] = jnp.zeros_like(coef_ref)

    row_g = lax.broadcasted_iota(jnp.int32, (rows, gs), 0) // nv
    row_c = lax.broadcasted_iota(jnp.int32, (rows, bands), 0) // nv
    row_v = lax.rem(lax.broadcasted_iota(jnp.int32, (rows, LANES), 0), nv)
    lane = lax.broadcasted_iota(jnp.int32, (rows, LANES), 1)

    def densities(x):
        high = x.astype(jnp.bfloat16).astype(jnp.float32)
        both = jnp.concatenate([high, x - high], axis=0).astype(jnp.bfloat16)
        top = jnp.zeros((rows, gs), jnp.float32)
        low = jnp.zeros((rows, gs), jnp.float32)
        for k in range(kl):
            res = jnp.dot(both, right[k], preferred_element_type=jnp.float32)
            top = jnp.where(row_g == k, res[:rows], top)
            low = jnp.where(row_g == k, res[rows:], low)
        return top, low

    def sums_tile(vec, applied):
        cross = jnp.sum(vec * applied, axis=1, keepdims=True)
        square = jnp.sum(applied * applied, axis=1, keepdims=True)
        own = jnp.sum(vec * vec, axis=1, keepdims=True)
        return jnp.where(lane == 0, cross, jnp.where(lane == 1, square, own))

    def coefficients(tile, turn):
        sums = jnp.zeros_like(tile)
        for v in range(nv):
            chain = jnp.sum(jnp.where(row_v == v, tile, 0.0), axis=0, keepdims=True)
            sums = jnp.where(row_v == v, chain, sums)
        alpha = sums[:, 0:1] / entries
        mean = sums[:, 1:2] / entries - 2.0 * alpha * alpha + alpha * alpha * (sums[:, 2:3] / entries)
        beta = jnp.sqrt(mean + epsilon)
        coef = jnp.where(lane == turn, alpha, coef_ref[...])
        coef_ref[...] = jnp.where(lane == STEPS + turn, beta, coef)
        return alpha, beta

    def advance(alpha, beta):
        vec = vec_ref[...]
        early_ref[...] = vec
        vec_ref[...] = (applied_ref[...] - alpha * vec) / beta

    beta_before = beta_ref[:, 0:1]
    right_copy.wait()
    for turn in range(STEPS):
        if turn == 0:
            top, low = densities(vec_ref[...])
            first[kme] = jnp.concatenate([top, top + low], axis=1)
            send_all(first, "kpt", nkp, kme, kdens_s.at[turn], kdens_r.at[turn])
            wait_all(first, "kpt", nkp, kme, kdens_s.at[turn], kdens_r.at[turn])
            blocks = []
            for s in range(nkp):
                blocks.append(first[s][:, :gs])
                dfull[s] = first[s][:, gs:]
        else:
            applied = applied_ref[...]
            top, low = densities(applied)
            mine = later.at[turn - 1]
            mine[kme] = jnp.concatenate([top + low, sums_tile(vec_ref[...], applied)], axis=1)
            send_all(mine, "kpt", nkp, kme, kdens_s.at[turn], kdens_r.at[turn])
            wait_all(mine, "kpt", nkp, kme, kdens_s.at[turn], kdens_r.at[turn])
            alpha, beta = coefficients(sum(mine[s][:, gs:] for s in range(nkp)), turn - 1)
            blocks = []
            for s in range(nkp):
                block = (mine[s][:, :gs] - alpha * dfull[s]) / beta
                dfull[s] = block
                blocks.append(block)
        gathered = dens.at[turn]
        gathered[pme] = jnp.concatenate(blocks, axis=0).astype(jnp.bfloat16)
        send_all(gathered, "pw", npw, pme, gdens_s.at[turn], gdens_r.at[turn])
        if turn > 0:
            advance(alpha, beta)
            beta_before = beta
        acc[...] = jnp.zeros_like(acc)

        def chunk_step(i, carry):
            @pl.when(i > 0)
            def _():
                arrival(
                    gathered, "pw", npw, pme, i, gdens_s.at[turn], gdens_r.at[turn]
                ).wait_recv()

            if turn == 0:
                screened_copy(i).wait()
            chunk = partner(pme, i, npw)
            picked = jnp.dot(
                choose_ref[...], gathered[chunk], preferred_element_type=jnp.float32
            ).astype(jnp.bfloat16)
            part = acc[...]
            for q in range(kl):
                part = part + lax.dot_general(
                    picked[q * total : (q + 1) * total],
                    screened[chunk, q],
                    (((1,), (1,)), ((), ())),
                    preferred_element_type=jnp.float32,
                )
            acc[...] = part
            return carry

        lax.fori_loop(0, npw, chunk_step, 0)
        out = held.at[turn]
        for s in range(nkp):
            out[s] = acc[s * rows : (s + 1) * rows, :]
        mine = fields.at[turn]
        for i in range(1, nkp):
            copy = exchange(
                mine, "kpt", nkp, kme, i, field_s.at[turn], field_r.at[turn],
                src=out.at[partner(kme, i, nkp)],
            )
            copy.start()
            pending.append(copy)
        mine[kme] = out[kme]
        if turn == 0:
            left_copy.wait()
        wait_all(mine, "kpt", nkp, kme, field_s.at[turn], field_r.at[turn])
        field = sum(mine[s] for s in range(nkp)).astype(jnp.bfloat16)
        part = jnp.zeros((rows, bands), jnp.float32)
        for k in range(kl):
            res = lax.dot_general(
                field, left[k], (((1,), (1,)), ((), ())), preferred_element_type=jnp.float32
            )
            part = jnp.where(row_c == k, res, part)
        mine = directs.at[turn]
        mine[pme] = part
        send_all(mine, "pw", npw, pme, direct_s.at[turn], direct_r.at[turn])
        wait_all(mine, "pw", npw, pme, direct_s.at[turn], direct_r.at[turn])
        direct = sum(mine[s] for s in range(npw))
        applied_ref[...] = (
            energy_ref[...] * vec_ref[...] - direct - beta_before * early_ref[...]
        )
    final[kme] = sums_tile(vec_ref[...], applied_ref[...])
    send_all(final, "kpt", nkp, kme, final_s, final_r)
    wait_all(final, "kpt", nkp, kme, final_s, final_r)
    alpha, beta = coefficients(sum(final[s] for s in range(nkp)), STEPS - 1)
    advance(alpha, beta)
    for copy in pending:
        copy.wait_send()


def on_device(
    nkp, npw,
    energies, current, previous, previous_beta, pair_left, pair_right, screened, momentum_index
):
    nv, kl, width = current.shape
    bands = pair_left.shape[1]
    gs = pair_left.shape[2]
    qcount = screened.shape[0]
    rows = kl * nv
    total = rows * nkp
    kme = lax.axis_index("kpt")
    pme = lax.axis_index("pw")
    to_rows = lambda a: jnp.transpose(a, (1, 0, 2)).reshape(rows, width)
    levels = jnp.broadcast_to(energies[:, None], (kl, nv, width)).reshape(rows, width)
    block = jnp.concatenate([to_rows(current), to_rows(previous), levels], axis=0)
    per = LANES // width
    spot = (jnp.arange(per) == pme % per)[None, :, None]
    packed = jnp.where(spot, block[:, None, :], 0.0).reshape(3 * rows, LANES)
    beta_rows = jnp.broadcast_to(jnp.tile(previous_beta, kl)[:, None], (rows, LANES))
    qpoints = kme * qcount + jnp.arange(qcount, dtype=jnp.int32)
    select = momentum_index[None] == qpoints[:, None, None]
    same = jnp.eye(nv, dtype=bool)
    choose = (select[:, :, None, :, None] & same[None, None, :, None, :]).astype(jnp.bfloat16)
    choose = choose.reshape(qcount * total, total)

    f32, bf16 = jnp.float32, jnp.bfloat16
    vmem = pl.BlockSpec(memory_space=pltpu.VMEM)
    hbm = pl.BlockSpec(memory_space=pl.ANY)
    dma = pltpu.SemaphoreType.DMA
    vec, early, coef = pl.pallas_call(
        functools.partial(kernel, (nkp, npw, kl, nv, bands, gs)),
        out_shape=(
            jax.ShapeDtypeStruct((rows, bands), f32),
            jax.ShapeDtypeStruct((rows, bands), f32),
            jax.ShapeDtypeStruct((rows, LANES), f32),
        ),
        in_specs=[vmem, vmem, vmem, hbm, hbm, hbm],
        out_specs=(vmem, vmem, vmem),
        scratch_shapes=[
            pltpu.VMEM((kl, bands, gs), bf16),
            pltpu.VMEM((kl, bands, gs), bf16),
            pltpu.VMEM((npw, qcount, gs, gs), bf16),
            pltpu.VMEM((npw, 3 * rows, LANES), f32),
            pltpu.VMEM((nkp, rows, 2 * gs), f32),
            pltpu.VMEM((STEPS - 1, nkp, rows, gs + LANES), f32),
            pltpu.VMEM((nkp, rows, LANES), f32),
            pltpu.VMEM((STEPS, npw, total, gs), bf16),
            pltpu.VMEM((rows, LANES), f32),
            pltpu.VMEM((STEPS, nkp, rows, gs), f32),
            pltpu.VMEM((STEPS, nkp, rows, gs), f32),
            pltpu.VMEM((STEPS, npw, rows, bands), f32),
            pltpu.VMEM((nkp, rows, gs), f32),
            pltpu.VMEM((rows, bands), f32),
            pltpu.VMEM((rows, bands), f32),
            pltpu.VMEM((total, gs), f32),
            dma, dma, dma((npw,)),
            dma((npw,)), dma((npw,)),
            dma((STEPS, nkp)), dma((STEPS, nkp)),
            dma((STEPS, npw)), dma((STEPS, npw)),
            dma((STEPS, nkp)), dma((STEPS, nkp)),
            dma((STEPS, npw)), dma((STEPS, npw)),
            dma((nkp,)), dma((nkp,)),
        ],
        compiler_params=pltpu.CompilerParams(
            collective_id=0, has_side_effects=True, vmem_limit_bytes=48 * 1024 * 1024
        ),
    )(packed, beta_rows, choose, pair_right, pair_left, screened)

    def own(a):
        a = jnp.transpose(a.reshape(kl, nv, bands), (1, 0, 2))
        return lax.dynamic_slice_in_dim(a, pme * width, width, 2)

    return own(vec), own(early), coef[:nv, :STEPS], coef[:nv, STEPS : 2 * STEPS]


def solution(mesh):
    return jax.shard_map(
        functools.partial(on_device, mesh.shape["kpt"], mesh.shape["pw"]),
        mesh=mesh,
        in_specs=(
            P("kpt", "pw"),
            P(None, "kpt", "pw"),
            P(None, "kpt", "pw"),
            P(),
            P("kpt", None, "pw"),
            P("kpt", None, "pw"),
            P("kpt", "pw", None),
            P(),
        ),
        out_specs=(P(None, "kpt", "pw"), P(None, "kpt", "pw"), P(), P()),
        check_vma=False,
    )
```

time: 436 us -> 88.2 us (0.20)
  blocking collectives: 276 us -> 0 us
  waiting for transfers between devices: 88.9 us -> 0 us
  Pallas kernels: 0 us -> 77 us
  matrix products: 41.3 us -> 0 us
  between operations: 14.7 us -> 0.7 us
    all_gather x9 -> x0, blocking collectives: 115 us -> none  [the longest x3 45.6 us: on_device(): rounded = lax.all_gather(rounded, 'pw', axis=2, tiled=True)]
    psum x3 -> x0, blocking collectives: 114 us -> none  [on_device(): lax.psum((jnp.sum(vector_own * applied, axis=(1, 2)), jnp.sum(applied * a...]
    unnamed x6 -> x0, waiting for transfers between devices: 88.9 us -> none
    pallas_call x0 -> x1, Pallas kernels: none -> 77 us  [on_device(): pl.pallas_call(functools.partial(kernel, (nkp, npw, kl, nv, bands, gs)),...]
    unnamed x3 -> x0, blocking collectives: 48.1 us -> none
    dot_general x12 -> x0, matrix products: 41.3 us -> none  [the longest x3 32.4 us: screened_images(): jnp.einsum('qsg,kvg->qkvs', screened, lax.all_gather(kpoint_rows, 'pw', a...]
    unnamed x28 -> x7, local copies, waits for them, and re-layouts: 9.32 us -> 5.14 us
  transfers between devices with their start and end apart: 3 -> 0, of which waited for: 3 -> 0; matrix products, arithmetic and copies ran while one was open for 0% -> 0% of each run, Pallas kernels for 0% -> 0%
where the time goes in v1:
time: 88.2 us; the launch traced here: 87.9 us
  Pallas kernels  77 us (87%)
  local copies, waits for them, and re-layouts  9.82 us (11%)
    pallas_call x1, Pallas kernels, on_device(): pl.pallas_call(functools.partial(kernel, (nkp, npw, kl, nv, bands, gs)),...  77 us
    unnamed x7, local copies, waits for them, and re-layouts  5.14 us

profile of v1, /device:TPU:0, one launch (start us, length us, event | category | flops | bytes accessed | tf_op | source)
XLA Modules:
  0.0 87.9 jit_solution(8794634735795988480)
XLA Ops:
  0.7 0.1 broadcast_in_dim.45
  0.7 0.1 broadcast_in_dim.46
  0.8 0.7 copy.14
  1.5 0.7 copy.15
  2.2 0.7 broadcast_in_dim.48
  2.9 0.1 broadcast_in_dim.50
  3.0 0.8 copy.16
  3.8 0.1 broadcast_compare_fusion
  3.9 0.2 and_convert_fusion
  4.1 0.7 reshape.58
  4.8 0.1 copy.17.choose_ref
  4.9 0.7 tile.2
  5.6 0.1 broadcast_in_dim.52
  5.6 0.1 broadcast_in_dim.53.beta_ref
  5.7 0.0 copy-start
  5.7 1.6 %copy-done = bf16[4,512,512]{2,1,0:T(8,128)(2,1)S(1)} copy-done((bf16[4,512,512]{2,1,0:T(8,128)(2,1)S(1)}, bf16[4,512,512]{2,1,0:T(8,128)(2,1)}, u32[]{:S(2)}) %copy-start) | copy-done | bytes 2097176
  7.3 0.0 copy-start.1
  7.3 1.6 %copy-done.1 = bf16[4,512,512]{2,1,0:T(8,128)(2,1)S(1)} copy-done((bf16[4,512,512]{2,1,0:T(8,128)(2,1)S(1)}, bf16[4,512,512]{2,1,0:T(8,128)(2,1)}, u32[]{:S(2)}) %copy-start.1) | copy-done | bytes 2097176
  8.9 77.0 %shard_map.111 = (f32[8,512]{1,0:T(8,128)S(1)}, f32[8,512]{1,0:T(8,128)S(1)}, f32[8,128]{1,0:T(8,128)S(1)}) custom-call(f32[24,128]{1,0:T(8,128)S(1)} %broadcast_select_fusion.packed_ref, f32[8,128]{1,0:T(8,128)S(1)} %broadcast_in_dim.53.beta_ref, bf16[128,32]{1,0:T(8,128)(2,1)S(1)} %copy.17.choose_ref, bf16[4,512,512]{2,1,0:T(8,128)(2,1)S(1)} %copy-done, ...), custom_call_target="tpu_custom_call" | custom-call | tf_op jit(solution)/shard_map/pallas_call | solution.py:280
  86.0 0.1 constant_dynamic-slice_fusion
  86.1 0.6 copy.24
  86.7 0.6 copy.25
  87.2 0.6 fusion
  (8 shorter events, 0.1 us)
Async XLA Ops:
  5.7 1.6 %copy-start = (bf16[4,512,512]{2,1,0:T(8,128)(2,1)S(1)}, bf16[4,512,512]{2,1,0:T(8,128)(2,1)}, u32[]{:S(2)}) copy-start(bf16[4,512,512]{2,1,0:T(8,128)(2,1)} %right_hbm.1) | copy-start | bytes 6291460
  7.3 1.6 %copy-start.1 = (bf16[4,512,512]{2,1,0:T(8,128)(2,1)S(1)}, bf16[4,512,512]{2,1,0:T(8,128)(2,1)}, u32[]{:S(2)}) copy-start(bf16[4,512,512]{2,1,0:T(8,128)(2,1)} %left_hbm.1) | copy-start | bytes 6291460

commit v2 on v1

--- a/solution.py
+++ b/solution.py
@@ -48,12 +48,13 @@
 
 def kernel(
     dims,
-    packed_ref, beta_ref, choose_ref, right_hbm, left_hbm, screened_hbm,
-    vec_ref, early_ref, coef_ref,
-    right, left, screened, packs, first, later, final, dens, images, held, fields, directs,
-    dfull, applied_ref, energy_ref, acc,
+    energies_ref, current_ref, previous_ref, beta_ref, index_ref,
+    right_hbm, left_hbm, screened_hbm,
+    last_ref, prior_ref, alphas_ref, betas_ref,
+    right, left, screened, packs, first, later, final, dens, held, fields, directs,
+    dfull, vec_ref, early_ref, coef_ref, applied_ref, energy_ref, choose_ref, acc,
     right_sem, left_sem, screened_sem,
-    pack_s, pack_r, kdens_s, kdens_r, gdens_s, gdens_r, field_s, field_r,
+    pack_s, pack_r, full_s, full_r, kdens_s, kdens_r, gdens_s, gdens_r, field_s, field_r,
     direct_s, direct_r, final_s, final_r,
 ):
     nkp, npw, kl, nv, bands, gs = dims
@@ -85,7 +86,19 @@
                 barrier, inc=1, device_id={axis: partner(me, i, n)},
                 device_id_type=pl.DeviceIdType.MESH,
             )
-    packs[pme] = packed_ref[...]
+    width = energies_ref.shape[1]
+    per = LANES // width
+    levels = energies_ref[...]
+    block = jnp.concatenate(
+        [current_ref[v] for v in range(nv)]
+        + [previous_ref[v] for v in range(nv)]
+        + [levels for v in range(nv)],
+        axis=0,
+    )
+    turn_at = lax.rem(pme, per)
+    packs[pme] = jnp.concatenate(
+        [block * (turn_at == j).astype(jnp.float32) for j in range(per)], axis=1
+    )
     pl.semaphore_wait(barrier, nkp - 1 + npw - 1)
 
     pending = []
@@ -101,9 +114,28 @@
             arrival(buf, axis, n, me, i, ssem, rsem).wait_recv()
 
     send_all(packs, "pw", npw, pme, pack_s, pack_r)
+
+    points = nkp * kl
+    row = lax.broadcasted_iota(jnp.int32, (total, points), 0)
+    col = lax.broadcasted_iota(jnp.int32, (total, points), 1)
+    point = (row // rows) * kl + lax.rem(row, kl)
+    spread = (point == col).astype(jnp.bfloat16)
+    index = index_ref[...].astype(jnp.float32).astype(jnp.bfloat16)
+    wide = jnp.dot(spread, index, preferred_element_type=jnp.float32).astype(jnp.bfloat16)
+    wide = lax.dot_general(
+        wide, spread, (((1,), (1,)), ((), ())), preferred_element_type=jnp.float32
+    )
+    chain_row = lax.rem(lax.broadcasted_iota(jnp.int32, (total, total), 0), rows) // kl
+    chain_col = lax.rem(lax.broadcasted_iota(jnp.int32, (total, total), 1), rows) // kl
+    same = (chain_row == chain_col).astype(jnp.float32)
+    for q in range(kl):
+        transfer = (kme * kl + q).astype(jnp.float32)
+        choose_ref[q * total : (q + 1) * total, :] = (
+            same * jnp.maximum(1.0 - jnp.abs(wide - transfer), 0.0)
+        ).astype(jnp.bfloat16)
+
     wait_all(packs, "pw", npw, pme, pack_s, pack_r)
 
-    per = npw * LANES // bands
     whole = jnp.concatenate(
         [sum(packs[m * per + j] for j in range(per)) for m in range(bands // LANES)], axis=1
     )
@@ -112,9 +144,10 @@
     energy_ref[...] = whole[2 * rows :]
     coef_ref[...] = jnp.zeros_like(coef_ref)
 
-    row_g = lax.broadcasted_iota(jnp.int32, (rows, gs), 0) // nv
-    row_c = lax.broadcasted_iota(jnp.int32, (rows, bands), 0) // nv
-    row_v = lax.rem(lax.broadcasted_iota(jnp.int32, (rows, LANES), 0), nv)
+    row_g = lax.broadcasted_iota(jnp.int32, (rows, gs), 0)
+    row_g = lax.rem(row_g, kl)
+    row_c = lax.rem(lax.broadcasted_iota(jnp.int32, (rows, bands), 0), kl)
+    row_v = lax.broadcasted_iota(jnp.int32, (rows, LANES), 0) // kl
     lane = lax.broadcasted_iota(jnp.int32, (rows, LANES), 1)
 
     def densities(x):
@@ -151,18 +184,18 @@
         early_ref[...] = vec
         vec_ref[...] = (applied_ref[...] - alpha * vec) / beta
 
-    beta_before = beta_ref[:, 0:1]
+    beta_before = jnp.zeros((rows, 1), jnp.float32)
+    for v in range(nv):
+        beta_before = jnp.where(row_v[:, 0:1] == v, beta_ref[v], beta_before)
     right_copy.wait()
     for turn in range(STEPS):
         if turn == 0:
             top, low = densities(vec_ref[...])
-            first[kme] = jnp.concatenate([top, top + low], axis=1)
+            first[kme] = top.astype(jnp.bfloat16)
             send_all(first, "kpt", nkp, kme, kdens_s.at[turn], kdens_r.at[turn])
+            dfull[kme] = top + low
             wait_all(first, "kpt", nkp, kme, kdens_s.at[turn], kdens_r.at[turn])
-            blocks = []
-            for s in range(nkp):
-                blocks.append(first[s][:, :gs])
-                dfull[s] = first[s][:, gs:]
+            blocks = [first[s].astype(jnp.float32) for s in range(nkp)]
         else:
             applied = applied_ref[...]
             top, low = densities(applied)
@@ -170,6 +203,10 @@
             mine[kme] = jnp.concatenate([top + low, sums_tile(vec_ref[...], applied)], axis=1)
             send_all(mine, "kpt", nkp, kme, kdens_s.at[turn], kdens_r.at[turn])
             wait_all(mine, "kpt", nkp, kme, kdens_s.at[turn], kdens_r.at[turn])
+            if turn == 1:
+                wait_all(dfull, "kpt", nkp, kme, full_s, full_r)
+                for copy in full_copies:
+                    copy.wait_send()
             alpha, beta = coefficients(sum(mine[s][:, gs:] for s in range(nkp)), turn - 1)
             blocks = []
             for s in range(nkp):
@@ -178,19 +215,23 @@
                 blocks.append(block)
         gathered = dens.at[turn]
         gathered[pme] = jnp.concatenate(blocks, axis=0).astype(jnp.bfloat16)
-        send_all(gathered, "pw", npw, pme, gdens_s.at[turn], gdens_r.at[turn])
+        gsend, grecv = gdens_s.at[turn], gdens_r.at[turn]
+        for i in [1] + list(range(2, npw, 2)):
+            copy = exchange(gathered, "pw", npw, pme, i, gsend, grecv)
+            copy.start()
+            pending.append(copy)
+        if turn == 0:
+            full_copies = []
+            for i in range(1, nkp):
+                copy = exchange(dfull, "kpt", nkp, kme, i, full_s, full_r)
+                copy.start()
+                full_copies.append(copy)
         if turn > 0:
             advance(alpha, beta)
             beta_before = beta
         acc[...] = jnp.zeros_like(acc)
 
-        def chunk_step(i, carry):
-            @pl.when(i > 0)
-            def _():
-                arrival(
-                    gathered, "pw", npw, pme, i, gdens_s.at[turn], gdens_r.at[turn]
-                ).wait_recv()
-
+        def product(i):
             if turn == 0:
                 screened_copy(i).wait()
             chunk = partner(pme, i, npw)
@@ -206,12 +247,39 @@
                     preferred_element_type=jnp.float32,
                 )
             acc[...] = part
+
+        def forward(i):
+            slot = partner(pme, i, npw)
+            return pltpu.make_async_remote_copy(
+                src_ref=gathered.at[slot],
+                dst_ref=gathered.at[slot],
+                send_sem=gsend.at[i + 1],
+                recv_sem=grecv.at[i + 1],
+                device_id={"pw": partner(pme, 1, npw)},
+                device_id_type=pl.DeviceIdType.MESH,
+            )
+
+        def near_step(p, carry):
+            i = 2 * p
+            arrival(gathered, "pw", npw, pme, i, gsend, grecv).wait_recv()
+            forward(i).start()
+            product(i)
             return carry
 
-        lax.fori_loop(0, npw, chunk_step, 0)
+        def far_step(p, carry):
+            i = 2 * p + 1
+            arrival(gathered, "pw", npw, pme, i, gsend, grecv).wait_recv()
+            product(i)
+            return carry
+
+        product(0)
+        far_step(0, 0)
+        lax.fori_loop(1, npw // 2, near_step, 0)
+        lax.fori_loop(1, npw // 2, far_step, 0)
+        pending += [forward(i) for i in range(2, npw, 2)]
         out = held.at[turn]
         for s in range(nkp):
-            out[s] = acc[s * rows : (s + 1) * rows, :]
+            out[s] = acc[s * rows : (s + 1) * rows, :].astype(jnp.bfloat16)
         mine = fields.at[turn]
         for i in range(1, nkp):
             copy = exchange(
@@ -224,7 +292,7 @@
         if turn == 0:
             left_copy.wait()
         wait_all(mine, "kpt", nkp, kme, field_s.at[turn], field_r.at[turn])
-        field = sum(mine[s] for s in range(nkp)).astype(jnp.bfloat16)
+        field = sum(mine[s].astype(jnp.float32) for s in range(nkp)).astype(jnp.bfloat16)
         part = jnp.zeros((rows, bands), jnp.float32)
         for k in range(kl):
             res = lax.dot_general(
@@ -232,10 +300,10 @@
             )
             part = jnp.where(row_c == k, res, part)
         mine = directs.at[turn]
-        mine[pme] = part
+        mine[pme] = part.astype(jnp.bfloat16)
         send_all(mine, "pw", npw, pme, direct_s.at[turn], direct_r.at[turn])
         wait_all(mine, "pw", npw, pme, direct_s.at[turn], direct_r.at[turn])
-        direct = sum(mine[s] for s in range(npw))
+        direct = sum(mine[s].astype(jnp.float32) for s in range(npw))
         applied_ref[...] = (
             energy_ref[...] * vec_ref[...] - direct - beta_before * early_ref[...]
         )
@@ -244,6 +312,15 @@
     wait_all(final, "kpt", nkp, kme, final_s, final_r)
     alpha, beta = coefficients(sum(final[s] for s in range(nkp)), STEPS - 1)
     advance(alpha, beta)
+    for source, target in ((vec_ref, last_ref), (early_ref, prior_ref)):
+        own = jnp.zeros((rows, width), jnp.float32)
+        for m in range(npw):
+            own = jnp.where(pme == m, source[:, m * width : (m + 1) * width], own)
+        for v in range(nv):
+            target[v] = own[v * kl : (v + 1) * kl]
+    for v in range(nv):
+        alphas_ref[v : v + 1, :] = coef_ref[v * kl : v * kl + 1, :STEPS]
+        betas_ref[v : v + 1, :] = coef_ref[v * kl : v * kl + 1, STEPS : 2 * STEPS]
     for copy in pending:
         copy.wait_send()
 
@@ -258,53 +335,44 @@
     qcount = screened.shape[0]
     rows = kl * nv
     total = rows * nkp
-    kme = lax.axis_index("kpt")
-    pme = lax.axis_index("pw")
-    to_rows = lambda a: jnp.transpose(a, (1, 0, 2)).reshape(rows, width)
-    levels = jnp.broadcast_to(energies[:, None], (kl, nv, width)).reshape(rows, width)
-    block = jnp.concatenate([to_rows(current), to_rows(previous), levels], axis=0)
-    per = LANES // width
-    spot = (jnp.arange(per) == pme % per)[None, :, None]
-    packed = jnp.where(spot, block[:, None, :], 0.0).reshape(3 * rows, LANES)
-    beta_rows = jnp.broadcast_to(jnp.tile(previous_beta, kl)[:, None], (rows, LANES))
-    qpoints = kme * qcount + jnp.arange(qcount, dtype=jnp.int32)
-    select = momentum_index[None] == qpoints[:, None, None]
-    same = jnp.eye(nv, dtype=bool)
-    choose = (select[:, :, None, :, None] & same[None, None, :, None, :]).astype(jnp.bfloat16)
-    choose = choose.reshape(qcount * total, total)
-
     f32, bf16 = jnp.float32, jnp.bfloat16
     vmem = pl.BlockSpec(memory_space=pltpu.VMEM)
-    hbm = pl.BlockSpec(memory_space=pl.ANY)
+    hbm = pl.BlockSpec(memory_space=pltpu.HBM)
+    smem = pl.BlockSpec(memory_space=pltpu.SMEM)
     dma = pltpu.SemaphoreType.DMA
-    vec, early, coef = pl.pallas_call(
+    return pl.pallas_call(
         functools.partial(kernel, (nkp, npw, kl, nv, bands, gs)),
         out_shape=(
-            jax.ShapeDtypeStruct((rows, bands), f32),
-            jax.ShapeDtypeStruct((rows, bands), f32),
-            jax.ShapeDtypeStruct((rows, LANES), f32),
+            jax.ShapeDtypeStruct(current.shape, f32),
+            jax.ShapeDtypeStruct(current.shape, f32),
+            jax.ShapeDtypeStruct((nv, STEPS), f32),
+            jax.ShapeDtypeStruct((nv, STEPS), f32),
         ),
-        in_specs=[vmem, vmem, vmem, hbm, hbm, hbm],
-        out_specs=(vmem, vmem, vmem),
+        in_specs=[vmem, vmem, vmem, smem, vmem, hbm, hbm, hbm],
+        out_specs=(vmem, vmem, vmem, vmem),
         scratch_shapes=[
             pltpu.VMEM((kl, bands, gs), bf16),
             pltpu.VMEM((kl, bands, gs), bf16),
             pltpu.VMEM((npw, qcount, gs, gs), bf16),
             pltpu.VMEM((npw, 3 * rows, LANES), f32),
-            pltpu.VMEM((nkp, rows, 2 * gs), f32),
+            pltpu.VMEM((nkp, rows, gs), bf16),
             pltpu.VMEM((STEPS - 1, nkp, rows, gs + LANES), f32),
             pltpu.VMEM((nkp, rows, LANES), f32),
             pltpu.VMEM((STEPS, npw, total, gs), bf16),
-            pltpu.VMEM((rows, LANES), f32),
-            pltpu.VMEM((STEPS, nkp, rows, gs), f32),
-            pltpu.VMEM((STEPS, nkp, rows, gs), f32),
-            pltpu.VMEM((STEPS, npw, rows, bands), f32),
+            pltpu.VMEM((STEPS, nkp, rows, gs), bf16),
+            pltpu.VMEM((STEPS, nkp, rows, gs), bf16),
+            pltpu.VMEM((STEPS, npw, rows, bands), bf16),
             pltpu.VMEM((nkp, rows, gs), f32),
             pltpu.VMEM((rows, bands), f32),
             pltpu.VMEM((rows, bands), f32),
+            pltpu.VMEM((rows, LANES), f32),
+            pltpu.VMEM((rows, bands), f32),
+            pltpu.VMEM((rows, bands), f32),
+            pltpu.VMEM((qcount * total, total), bf16),
             pltpu.VMEM((total, gs), f32),
             dma, dma, dma((npw,)),
             dma((npw,)), dma((npw,)),
+            dma((nkp,)), dma((nkp,)),
             dma((STEPS, nkp)), dma((STEPS, nkp)),
             dma((STEPS, npw)), dma((STEPS, npw)),
             dma((STEPS, nkp)), dma((STEPS, nkp)),
@@ -312,15 +380,12 @@
             dma((nkp,)), dma((nkp,)),
         ],
         compiler_params=pltpu.CompilerParams(
-            collective_id=0, has_side_effects=True, vmem_limit_bytes=48 * 1024 * 1024
+            collective_id=0, has_side_effects=True, vmem_limit_bytes=60 * 1024 * 1024
         ),
-    )(packed, beta_rows, choose, pair_right, pair_left, screened)
-
-    def own(a):
-        a = jnp.transpose(a.reshape(kl, nv, bands), (1, 0, 2))
-        return lax.dynamic_slice_in_dim(a, pme * width, width, 2)
-
-    return own(vec), own(early), coef[:nv, :STEPS], coef[:nv, STEPS : 2 * STEPS]
+    )(
+        energies, current, previous, previous_beta, momentum_index,
+        pair_right, pair_left, screened,
+    )
 
 
 def solution(mesh):

time: 88.2 us -> 81.1 us (0.920)
  local copies, waits for them, and re-layouts: 9.82 us -> 4.95 us
  Pallas kernels: 77 us -> 75.2 us
    pallas_call x1, Pallas kernels: 77 us -> 75.2 us  [on_device(): pl.pallas_call(functools.partial(kernel, (nkp, npw, kl, nv, bands, gs)),...]
    transpose x2 -> x0, local copies, waits for them, and re-layouts: 1.38 us -> none  [on_device(): to_rows = lambda a: jnp.transpose(a, (1, 0, 2)).reshape(rows, width)]
    broadcast_in_dim x7 -> x0, local copies, waits for them, and re-layouts: 1.1 us -> none  [the longest x1 0.68 us: on_device(): jnp.broadcast_to(energies[:, None], (kl, nv, width)).reshape(rows, width)]
    unnamed x7 -> x4, local copies, waits for them, and re-layouts: 5.14 us -> 4.95 us
where the time goes in v2:
time: 81.1 us; the launch traced here: 80.8 us
  Pallas kernels  75.2 us (93%)
  local copies, waits for them, and re-layouts  4.95 us (6%)
    pallas_call x1, Pallas kernels, on_device(): pl.pallas_call(functools.partial(kernel, (nkp, npw, kl, nv, bands, gs)),...  75.2 us
    unnamed x4, local copies, waits for them, and re-layouts  4.95 us

profile of v2, /device:TPU:0, one launch (start us, length us, event | category | flops | bytes accessed | tf_op | source)
XLA Modules:
  0.0 80.8 jit_solution(1337853641690010147)
XLA Ops:
  0.6 75.2 %shard_map.111 = (f32[2,4,64]{2,1,0:T(4,128)}, f32[2,4,64]{2,1,0:T(4,128)}, f32[2,3]{1,0:T(2,128)}, f32[2,3]{1,0:T(2,128)}) custom-call(f32[4,64]{1,0:T(4,128)} %energies_ref.1, f32[2,4,64]{2,1,0:T(4,128)} %current_ref.1, f32[2,4,64]{2,1,0:T(4,128)} %previous_ref.1, f32[2]{0:T(128)} %beta_ref.1, s32[16,16]{1,0:T(8,128)} %index_ref.1, ...), custom_call_target="tpu_custom_call" | custom-call | tf_op jit(solution)/shard_map/pallas_call | solution.py:343
  75.8 1.3 %copy.16 = f32[2,4,64]{2,1,0:T(4,128)} copy(f32[2,4,64]{2,1,0:T(4,128)} %get-tuple-element.8) | data formatting | bytes 4096
  77.1 1.3 %copy.17 = f32[2,4,64]{2,1,0:T(4,128)} copy(f32[2,4,64]{2,1,0:T(4,128)} %get-tuple-element.9) | data formatting | bytes 4096
  78.3 1.2 %copy.18 = f32[2,3]{1,0:T(2,128)} copy(f32[2,3]{1,0:T(2,128)} %get-tuple-element.10) | data formatting | bytes 48
  79.6 1.2 %copy.19 = f32[2,3]{1,0:T(2,128)} copy(f32[2,3]{1,0:T(2,128)} %get-tuple-element.11) | data formatting | bytes 48
